TPU v7x, 32 devices: a whole 2x2x4 slice. The times are simulated.
32 devices in a mesh: dp: 8 (over z, x), shard: 4 (over y, core).
Axes of the slice: x: 2, y: 2, z: 4, core: 2. Of those that a mesh axis runs over, the one named last changes fastest.
Arguments:
- hidden_in: bfloat16 [8192, 5120], P(('dp', 'shard')), may hold values from -6 to 6
- teacher: bfloat16 [8192, 768], P(('dp', 'shard')), may hold values from -6 to 6
- norm_gain: bfloat16 [5120], P('shard'), may hold values from 0.5 to 1.5
- w_key: bfloat16 [5120, 768], P('shard'), may hold values from -0.078125 to 0.078125
- group_rows: int32 [8], P('dp'), may hold values from 64 to 256
- member: int32 [8, 4], P('dp', 'shard'), may hold values from 0 to 1, as said below
Outputs:
- loss: float32 [], replicated
- grad_gain: float32 [5120], P('shard')
- grad_key: float32 [5120, 768], P('shard')
Inputs may be any that keep to these rules, and one draw needn't show every extreme that they name: The first group_rows[p] token slots of each surviving device of group p hold valid tokens. `member`: 1 marks a surviving device; the first device of every group survives.
All inputs are finite; a program needn't handle non-finite values.
Results may differ from a plain program's by a relative error of at most 0.0023.
Values may be sent and summed in bfloat16 or wider, within the bound.
A program may use at most 128 MiB of HBM per device.

v0:
```python
import functools
import math

import jax
import jax.numpy as jnp
from jax import lax
from jax.experimental import pallas as pl
from jax.experimental.pallas import tpu as pltpu
from jax.sharding import PartitionSpec as P

EPSILON = 1e-06
SCALE = 1024.0
MESH = pl.DeviceIdType.MESH
F32 = jnp.float32
BF16 = jnp.bfloat16


def inner_of(groups):
    return max(d for d in range(1, groups + 1) if groups % d == 0 and d * d <= groups)


def kernel(
    members, groups, width, chunks,
    hidden, teacher, gains, w_key, valid, count,
    out, loss_out,
    inv_cols, small_send, small_recv, cnt_send, cnt_recv, loss_send, loss_recv,
    cols, cols_t, part_send, part_recv, keys_own, keys_recv, dk_all,
    grads, x_send, x_recv, half, half_send, z_recv,
    a2a_s, a2a_r, small_s, small_r, cnt_s, cnt_r, loss_s, loss_r,
    part_s, part_r, keys_s, keys_r, dk_s, dk_r, dks_s, dks_r, dkf_s, dkf_r,
    x_s, x_r, z_s, z_r, zu_s, zd_s, za_r, xa_s, xa_r,
):
    tokens, kv = teacher.shape
    feats = w_key.shape[0]
    kc = kv // chunks
    inner = inner_of(groups)
    outer = groups // inner
    hrows = feats // inner
    qrows = hrows // outer
    pairs = members // 2
    align = 16
    p, s = lax.axis_index("dp"), lax.axis_index("shard")
    px, pz = lax.rem(p, inner), p // inner
    chip, par = s // 2, lax.rem(s, 2)
    twin = chip * 2 + 1 - par
    pending = []

    def member_at(d):
        return lax.rem(s + d, members)

    def group_at(d):
        return lax.rem(p + d, groups)

    def chip_at(d):
        return lax.rem(chip + d, pairs)

    def x_at(d):
        return lax.rem(px + d, inner)

    def z_at(d):
        return lax.rem(pz + d, outer)

    def send(src, dst, ssem, rsem, group, member):
        copy = pltpu.make_async_remote_copy(
            src_ref=src, dst_ref=dst, send_sem=ssem, recv_sem=rsem,
            device_id=(group, member), device_id_type=MESH,
        )
        copy.start()
        pending.append(copy)

    def arrived(dst, ssem, rsem):
        pltpu.make_async_remote_copy(
            src_ref=dst, dst_ref=dst, send_sem=ssem, recv_sem=rsem,
            device_id=(p, twin), device_id_type=MESH,
        ).wait_recv()

    barrier = pltpu.get_barrier_semaphore()
    for d in range(1, members):
        pl.semaphore_signal(barrier, inc=1, device_id=(p, member_at(d)), device_id_type=MESH)
    for d in range(1, groups):
        pl.semaphore_signal(barrier, inc=1, device_id=(group_at(d), s), device_id_type=MESH)
    pl.semaphore_wait(barrier, members + groups - 2)

    for d in range(1, members):
        j = member_at(d)
        send(
            hidden.at[:, pl.ds(pl.multiple_of(j * feats, 128), feats)],
            cols.at[s], a2a_s.at[d - 1], a2a_r.at[d - 1], p, j,
        )

    step_rows = 64
    def squares(r, carry):
        rows = pl.ds(pl.multiple_of(r * step_rows, step_rows), step_rows)
        x = hidden[rows, :].astype(F32)
        total = jnp.sum(x * x, axis=1, keepdims=True)
        inv = lax.rsqrt(total / width + EPSILON)
        inv_cols[rows, :] = jnp.broadcast_to(inv, (step_rows, 128))
        return carry
    lax.fori_loop(0, tokens // step_rows, squares, 0)

    small_send[pl.ds(0, 8), :] = inv_cols[...].T[:8, :]
    small_send[pl.ds(8, 8), :] = jnp.broadcast_to(count[:, :1], (8, tokens))
    for d in range(1, members):
        send(small_send, small_recv.at[d - 1], small_s.at[d - 1], small_r.at[d - 1], p, member_at(d))

    def normalise(j, source, column):
        def rows_of(r, carry):
            rows = pl.ds(pl.multiple_of(r * step_rows, step_rows), step_rows)
            x = source(rows).astype(F32) * inv_cols[rows, :1]
            cols[j, rows, :] = (x * gains[...]).astype(BF16)
            return carry
        lax.fori_loop(0, tokens // step_rows, rows_of, 0)

        def turn(b, carry):
            lanes = pl.ds(pl.multiple_of(b * 128, 128), 128)
            cols_t[lanes, pl.ds(pl.multiple_of(j * tokens, 128), tokens)] = cols[j, :, lanes].T
            return carry
        lax.fori_loop(0, feats // 128, turn, 0)

    own = pl.ds(pl.multiple_of(s * feats, 128), feats)
    normalise(s, lambda rows: hidden[rows, own], None)

    total = count[...]
    for d in range(1, members):
        arrived(small_recv.at[d - 1], small_s.at[d - 1], small_r.at[d - 1])
        total = total + small_recv[d - 1, pl.ds(8, 8), :128]
    cnt_send[...] = total
    for d in range(1, groups):
        send(cnt_send, cnt_recv.at[d - 1], cnt_s.at[d - 1], cnt_r.at[d - 1], group_at(d), s)

    for d in range(1, members):
        j = lax.rem(s + members - d, members)
        arrived(cols.at[j], a2a_s.at[d - 1], a2a_r.at[d - 1])
        inv_cols[...] = jnp.broadcast_to(small_recv[d - 1, pl.ds(0, 1), :], (128, tokens)).T
        normalise(j, lambda rows: cols[j, rows, :], None)

    for d in range(1, groups):
        arrived(cnt_recv.at[d - 1], cnt_s.at[d - 1], cnt_r.at[d - 1])
        total = total + cnt_recv[d - 1]
    scale = valid[...] * (SCALE / total[:1, :1])

    def lanes_of(c):
        return pl.ds(c * kc, kc)

    def stage_keys(c):
        for d in range(pairs):
            j = chip_at(d) * 2 + 1 - par
            part_send[c, d] = jnp.dot(cols[j], w_key[:, lanes_of(c)], preferred_element_type=F32)
            send(part_send.at[c, d], part_recv.at[c, d], part_s.at[c, d], part_r.at[c, d], p, twin)
        for i in range(pairs):
            d = (i + 1) % pairs
            j = chip_at(d) * 2 + par
            mine = jnp.dot(cols[j], w_key[:, lanes_of(c)], preferred_element_type=F32)
            arrived(part_recv.at[c, d], part_s.at[c, d], part_r.at[c, d])
            keys_own[c, d] = mine + part_recv[c, d]
            if d:
                send(
                    keys_own.at[c, d], keys_recv.at[c, d - 1],
                    keys_s.at[c, d - 1], keys_r.at[c, d - 1], p, j,
                )

    def stage_dk(c):
        keys = keys_own[c, 0]
        for d in range(1, pairs):
            arrived(keys_recv.at[c, d - 1], keys_s.at[c, d - 1], keys_r.at[c, d - 1])
            keys = keys + keys_recv[c, d - 1]
        diff = keys - teacher[:, lanes_of(c)].astype(F32)
        dk_all[c, s] = (scale * diff).astype(BF16)
        for d in range(1, pairs):
            send(
                dk_all.at[c, s], dk_all.at[c, s], dk_s.at[c, d - 1], dk_r.at[c, d - 1],
                p, chip_at(d) * 2 + par,
            )
        send(dk_all.at[c, s], dk_all.at[c, s], dks_s.at[c], dks_r.at[c], p, twin)

    def stage_grads(c, loss):
        for d in range(1, pairs):
            q = lax.rem(chip + pairs - d, pairs) * 2 + par
            arrived(dk_all.at[c, q], dk_s.at[c, d - 1], dk_r.at[c, d - 1])
            send(dk_all.at[c, q], dk_all.at[c, q], dkf_s.at[c, d - 1], dkf_r.at[c, d - 1], p, twin)
        arrived(dk_all.at[c, twin], dks_s.at[c], dks_r.at[c])
        for d in range(1, pairs):
            q = lax.rem(chip + pairs - d, pairs) * 2 + 1 - par
            arrived(dk_all.at[c, q], dkf_s.at[c, d - 1], dkf_r.at[c, d - 1])
        dk = dk_all[c].reshape(members * tokens, kc)
        for i in range(inner):
            d = (i + 1) % inner
            rows = pl.ds(pl.multiple_of(x_at(d) * hrows, 8), hrows)
            term = jnp.dot(cols_t[rows, :], dk, preferred_element_type=F32)
            if not d:
                grads[c] = term
            else:
                x_send[c, d - 1] = term.astype(BF16)
                send(
                    x_send.at[c, d - 1], x_recv.at[c, d - 1], x_s.at[c, d - 1], x_r.at[c, d - 1],
                    pz * inner + x_at(d), s,
                )
        for m in range(members):
            values = dk_all[c, m].astype(F32)
            loss = loss + jnp.sum(values * values, axis=0, keepdims=True)
        return loss

    def stage_z(c):
        value = grads[c]
        for d in range(1, inner):
            arrived(x_recv.at[c, d - 1], x_s.at[c, d - 1], x_r.at[c, d - 1])
            value = value + x_recv[c, d - 1].astype(F32)
        half[c] = value
        half_send[c] = value.astype(BF16)
        for d in range(1, outer):
            to = z_at(d)
            send(
                half_send.at[c, pl.ds(pl.multiple_of(to * qrows, align), qrows), :], z_recv.at[c, d - 1],
                z_s.at[c, d - 1], z_r.at[c, d - 1], to * inner + px, s,
            )

    def rows_at(x, z):
        return pl.ds(pl.multiple_of(x * hrows + z * qrows, 8), qrows)

    def stage_sum(c):
        value = half[c, pl.ds(pl.multiple_of(pz * qrows, 8), qrows), :]
        for d in range(1, outer):
            arrived(z_recv.at[c, d - 1], z_s.at[c, d - 1], z_r.at[c, d - 1])
            value = value + z_recv[c, d - 1].astype(F32)
        mine = rows_at(px, pz)
        out[mine, lanes_of(c)] = value
        spot = out.at[mine, lanes_of(c)]
        along_line(spot, c, pz)
        across(spot, c, pz)

    def across(spot, c, q):
        for e in range(1, inner):
            copy_to(spot, xa_s.at[c, e - 1, q], xa_r.at[c, e - 1, q], pz * inner + x_at(e), s).start()

    def copy_to(spot, ssem, rsem, group, member):
        return pltpu.make_async_remote_copy(
            src_ref=spot, dst_ref=spot, send_sem=ssem, recv_sem=rsem,
            device_id=(group, member), device_id_type=MESH,
        )

    def rises(q):
        return (pz >= q) & (pz < outer - 1)

    def falls(q):
        return (pz <= q) & (pz > 0)

    def up_copy(spot, c, q):
        to = jnp.minimum(pz + 1, outer - 1) * inner + px
        return copy_to(spot, zu_s.at[c, q], za_r.at[c, q], to, s)

    def down_copy(spot, c, q):
        to = jnp.maximum(pz - 1, 0) * inner + px
        return copy_to(spot, zd_s.at[c, q], za_r.at[c, q], to, s)

    def along_line(spot, c, q):
        @pl.when(rises(q))
        def _():
            up_copy(spot, c, q).start()

        @pl.when(falls(q))
        def _():
            down_copy(spot, c, q).start()

    def stage_spread(c):
        for q in range(outer):
            spot = out.at[rows_at(px, q), lanes_of(c)]

            @pl.when(pz != q)
            def _():
                arrived(spot, zu_s.at[c, q], za_r.at[c, q])
                along_line(spot, c, q)
                across(spot, c, q)

    loss = jnp.zeros((1, kc), F32)
    for step in range(chunks + 5):
        for lag, stage in enumerate((stage_keys, stage_dk, stage_grads, stage_z, stage_sum, stage_spread)):
            c = step - lag
            if 0 <= c < chunks:
                if stage is stage_grads:
                    loss = stage(c, loss)
                else:
                    stage(c)
        if step == chunks + 1:
            loss_send[...] = jnp.broadcast_to(jnp.sum(loss, axis=1, keepdims=True), (8, 128))
            for d in range(1, groups):
                send(loss_send, loss_recv.at[d - 1], loss_s.at[d - 1], loss_r.at[d - 1], group_at(d), s)

    square = loss_send[...]
    for d in range(1, groups):
        arrived(loss_recv.at[d - 1], loss_s.at[d - 1], loss_r.at[d - 1])
        square = square + loss_recv[d - 1]
    loss_out[...] = square * (total * (1.0 / (SCALE * SCALE * 2.0 * kv)))
    for c in range(chunks):
        for q in range(outer):
            for e in range(1, inner):
                spot = out.at[rows_at(lax.rem(px + inner - e, inner), q), lanes_of(c)]
                arrived(spot, xa_s.at[c, e - 1, q], xa_r.at[c, e - 1, q])
                spot = out.at[rows_at(px, q), lanes_of(c)]
                copy_to(spot, xa_s.at[c, e - 1, q], xa_r.at[c, e - 1, q], pz * inner + x_at(e), s).wait_send()
            spot = out.at[rows_at(px, q), lanes_of(c)]

            @pl.when(rises(q))
            def _():
                up_copy(spot, c, q).wait_send()

            @pl.when(falls(q))
            def _():
                down_copy(spot, c, q).wait_send()
    for copy in pending:
        copy.wait_send()


def body(members, groups, hidden_in, teacher, norm_gain, w_key, group_rows, member):
    tokens, width = hidden_in.shape
    owned, kv = w_key.shape
    unit = math.lcm(128, 16 * groups)
    feats = -(-owned // unit) * unit
    chunks = kv // 256 if kv % 256 == 0 else 1
    kc = kv // chunks
    live_rows, alive = group_rows[0], member[0, 0]
    position = lax.broadcasted_iota(jnp.int32, (tokens, 1), 0)
    valid = jnp.where((position < live_rows) & (alive == 1), 1.0, 0.0).astype(F32)
    count = jnp.broadcast_to((alive * live_rows).astype(F32), (8, 128))
    gains = norm_gain.astype(F32)
    hidden, weights, wide_gains = hidden_in, w_key, gains
    if feats != owned:
        extra = feats - owned
        hidden = jnp.pad(hidden_in.reshape(tokens, members, owned), ((0, 0), (0, 0), (0, extra)))
        hidden = hidden.reshape(tokens, members * feats)
        weights = jnp.pad(w_key, ((0, extra), (0, 0)))
        wide_gains = jnp.pad(gains, (0, extra))
    inner = inner_of(groups)
    outer = groups // inner
    hrows, pairs = feats // inner, members // 2
    vm = pltpu.VMEM

    def sems(*shape):
        kind = pltpu.SemaphoreType.DMA(tuple(max(n, 1) for n in shape))
        return [kind, kind]

    grad_key, loss = pl.pallas_call(
        functools.partial(kernel, members, groups, width, chunks),
        out_shape=(
            jax.ShapeDtypeStruct((feats, kv), F32),
            jax.ShapeDtypeStruct((8, 128), F32),
        ),
        in_specs=[pl.BlockSpec(memory_space=pltpu.VMEM)] * 6,
        out_specs=(pl.BlockSpec(memory_space=pltpu.VMEM),) * 2,
        scratch_shapes=[
            vm((tokens, 128), F32),
            vm((16, tokens), F32), vm((members - 1, 16, tokens), F32),
            vm((8, 128), F32), vm((groups - 1, 8, 128), F32),
            vm((8, 128), F32), vm((groups - 1, 8, 128), F32),
            vm((members, tokens, feats), BF16), vm((feats, members * tokens), BF16),
            vm((chunks, pairs, tokens, kc), F32), vm((chunks, pairs, tokens, kc), F32),
            vm((chunks, pairs, tokens, kc), F32), vm((chunks, max(pairs - 1, 1), tokens, kc), F32),
            vm((chunks, members, tokens, kc), BF16),
            vm((chunks, hrows, kc), F32),
            vm((chunks, max(inner - 1, 1), hrows, kc), BF16), vm((chunks, max(inner - 1, 1), hrows, kc), BF16),
            vm((chunks, hrows, kc), F32), vm((chunks, hrows, kc), BF16),
            vm((chunks, max(outer - 1, 1), hrows // outer, kc), BF16),
            *sems(members - 1), *sems(members - 1), *sems(groups - 1), *sems(groups - 1),
            *sems(chunks, pairs), *sems(chunks, pairs - 1), *sems(chunks, pairs - 1), *sems(chunks),
            *sems(chunks, pairs - 1),
            *sems(chunks, inner - 1), *sems(chunks, outer - 1),
            *sems(chunks, outer), sems(chunks, outer)[0], *sems(chunks, inner - 1, outer),
        ],
        compiler_params=pltpu.CompilerParams(
            collective_id=0, has_side_effects=True, vmem_limit_bytes=60 * 1024 * 1024
        ),
    )(hidden, teacher, wide_gains.reshape(1, feats), weights, valid, count)
    grad_key = grad_key[:owned]
    grad_gain = jnp.sum(grad_key * w_key.astype(F32), axis=1) / gains
    return (loss[0, 0], grad_gain, grad_key)


def solution(mesh):
    in_specs = (
        P(("dp", "shard"), None),
        P(("dp", "shard"), None),
        P("shard"),
        P("shard", None),
        P("dp"),
        P("dp", "shard"),
    )
    out_specs = (P(), P("shard"), P("shard", None))
    step = functools.partial(body, mesh.shape["shard"], mesh.shape["dp"])
    return jax.shard_map(step, mesh=mesh, in_specs=in_specs, out_specs=out_specs, check_vma=False)
```

profile of v0, /device:TPU:0, one launch (start us, length us, event | category | flops | bytes accessed | tf_op | source)
XLA Modules:
  0.0 159.8 jit_solution(8228425981901819659)
XLA Ops:
  0.6 0.0 copy-start.1
  2.1 0.6 broadcast_in_dim.13.count
  2.7 1.3 reshape.25.gains
  4.0 0.7 fusion.1.valid
  4.6 148.7 %shard_map.85 = (f32[1280,768]{1,0:T(8,128)}, f32[8,128]{1,0:T(8,128)}) custom-call(bf16[256,5120]{1,0:T(8,128)(2,1)} %hidden.1, bf16[256,768]{1,0:T(8,128)(2,1)} %teacher.1, f32[1,1280]{1,0:T(1,128)} %reshape.25.gains, bf16[1280,768]{1,0:T(8,128)(2,1)} %w_key.1, f32[256,1]{1,0:T(8,128)} %fusion.1.valid, f32[8,128]{1,0:T(8,128)} %broadcast_in_dim.13.count), custom_call_target="tpu_custom_call" | custom-call | tf_op jit(solution)/shard_map/pallas_call | solution.py:341
  153.3 0.0 copy-start.2
  153.3 0.0 copy-start
  153.3 1.3 slice.3
  154.7 0.0 copy-done.1
  154.7 2.6 %multiply_reduce_fusion = f32[1280]{0:T(1024)S(1)} fusion(f32[1280,768]{1,0:T(8,128)} %get-tuple-element.12, bf16[1280,768]{1,0:T(8,128)(2,1)S(1)} %copy-done.1), kind=kLoop, calls=%fused_computation | loop fusion | flops 2947840 | bytes 5903360 | tf_op jit(solution)/shard_map/reduce_sum | solution.py:373
  157.2 0.0 copy-done.2
  157.2 0.6 convert_divide_fusion
  157.9 0.0 copy-done
  157.9 1.9 %copy.12 = f32[1280,768]{1,0:T(8,128)} copy(f32[1280,768]{1,0:T(8,128)S(1)} %copy-done) | data formatting | bytes 7864320
Async XLA Ops:
  0.6 154.0 %copy-start.1 = (bf16[1280,768]{1,0:T(8,128)(2,1)S(1)}, bf16[1280,768]{1,0:T(8,128)(2,1)}, u32[]{:S(2)}) copy-start(bf16[1280,768]{1,0:T(8,128)(2,1)} %w_key.1) | copy-start | bytes 5898244
  153.3 3.9 %copy-start.2 = (bf16[1280]{0:T(1024)(128)(2,1)S(1)}, bf16[1280]{0:T(1024)(128)(2,1)}, u32[]{:S(2)}) copy-start(bf16[1280]{0:T(1024)(128)(2,1)} %param.8) | copy-start | bytes 7684
  153.3 4.5 %copy-start = (f32[1280,768]{1,0:T(8,128)S(1)}, f32[1280,768]{1,0:T(8,128)}, u32[]{:S(2)}) copy-start(f32[1280,768]{1,0:T(8,128)} %get-tuple-element.12) | copy-start | bytes 11796484
where the time goes:
time: 161 us; the launch traced here: 160 us
  Pallas kernels  149 us (93%)
  local copies, waits for them, and re-layouts  5.15 us (3%)
  other arithmetic  3.86 us (2%)
  between operations  2.11 us (1%)
    pallas_call x1, Pallas kernels, body(): pl.pallas_call(functools.partial(kernel, members, groups, width, chunks),...  149 us

commit v1 on v0

v1 whole, which is shorter than its diff:
```python
import functools
import math

import jax
import jax.numpy as jnp
from jax import lax
from jax.experimental import pallas as pl
from jax.experimental.pallas import tpu as pltpu
from jax.sharding import PartitionSpec as P

EPSILON = 1e-06
SCALE = 1024.0
MESH = pl.DeviceIdType.MESH
F32 = jnp.float32
BF16 = jnp.bfloat16


def inner_of(groups):
    return max(d for d in range(1, groups + 1) if groups % d == 0 and d * d <= groups)


def paired(index, k, size):
    if size & (size - 1):
        return None
    out, bit = 0, 1
    while bit < size:
        out = out + lax.rem(lax.rem(index // bit, 2) + (k // bit) % 2, 2) * bit
        bit *= 2
    return out


def kernel(
    members, groups, width, chunks,
    live_rows, alive, hidden_in, teacher, gains, w_in,
    out, loss_out,
    hidden, w_full, gains_all, cnt_m, cnt_g, loss_m, loss_g,
    n_own, n_recv, n_t, dk_all, grads,
    x_send, x_recv, z_near, z_near_recv, z_far, z_far_recv,
    load_s, gain_s, gain_r, cnt_s, cnt_r, cntg_s, cntg_r,
    loss_s, loss_r, lossg_s, lossg_r, wy_s, wy_r, wz_s, wz_r, wx_s, wx_r, wt_s, wt_r,
    n_s, n_r, dk_s, dk_r, dks_s, dks_r, dkf_s, dkf_r,
    x_s, x_r, z_s, z_r, az_s, az_r, ax_s, ax_r,
):
    tokens, kv = teacher.shape
    feats = w_in.shape[0]
    kc = kv // chunks
    inner = inner_of(groups)
    outer = groups // inner
    hrows = feats // inner
    qrows = hrows // outer
    pairs = members // 2
    p, s = lax.axis_index("dp"), lax.axis_index("shard")
    px, pz = lax.rem(p, inner), p // inner
    chip, par = s // 2, lax.rem(s, 2)
    twin = chip * 2 + 1 - par
    pending = []

    def member_at(d):
        return lax.rem(s + d, members)

    def group_at(d):
        return lax.rem(p + d, groups)

    def chip_at(d):
        return lax.rem(chip + d + pairs, pairs)

    def x_at(d):
        return lax.rem(px + d + inner, inner)

    def z_to(k):
        q = paired(pz, k, outer)
        return lax.rem(pz + k, outer) if q is None else q

    def z_from(k):
        q = paired(pz, k, outer)
        return lax.rem(pz + outer - k, outer) if q is None else q

    def send(src, dst, ssem, rsem, group, member):
        copy = pltpu.make_async_remote_copy(
            src_ref=src, dst_ref=dst, send_sem=ssem, recv_sem=rsem,
            device_id=(group, member), device_id_type=MESH,
        )
        copy.start()
        pending.append(copy)

    def arrived(dst, ssem, rsem):
        pltpu.make_async_remote_copy(
            src_ref=dst, dst_ref=dst, send_sem=ssem, recv_sem=rsem,
            device_id=(p, twin), device_id_type=MESH,
        ).wait_recv()

    def lanes_of(c):
        return pl.ds(c * kc, kc)

    def rows_at(x, z):
        return pl.ds(pl.multiple_of(x * hrows + z * qrows, 16), qrows)

    loads = [
        pltpu.make_async_copy(w_in.at[:, lanes_of(c)], w_full.at[c, s], load_s.at[c])
        for c in range(chunks)
    ]
    loads.append(pltpu.make_async_copy(hidden_in, hidden, load_s.at[chunks]))
    for copy in loads:
        copy.start()

    rows_count, is_alive = live_rows[0], alive[0, 0]
    gains_all[s] = gains[...]
    cnt_m[s] = jnp.broadcast_to((is_alive * rows_count).astype(F32), (8, 128))

    barrier = pltpu.get_barrier_semaphore()
    for d in range(1, members):
        pl.semaphore_signal(barrier, inc=1, device_id=(p, member_at(d)), device_id_type=MESH)
    for d in range(1, groups):
        pl.semaphore_signal(barrier, inc=1, device_id=(group_at(d), s), device_id_type=MESH)
    pl.semaphore_wait(barrier, members + groups - 2)

    def to_members(buf, ssem, rsem):
        for d in range(1, members):
            send(buf.at[s], buf.at[s], ssem.at[d - 1], rsem.at[d - 1], p, member_at(d))

    def from_members(buf, ssem, rsem):
        for d in range(1, members):
            j = lax.rem(s + members - d, members)
            arrived(buf.at[j], ssem.at[d - 1], rsem.at[d - 1])

    def to_groups(buf, ssem, rsem):
        for d in range(1, groups):
            send(buf.at[p], buf.at[p], ssem.at[d - 1], rsem.at[d - 1], group_at(d), s)

    def from_groups(buf, ssem, rsem):
        for d in range(1, groups):
            j = lax.rem(p + groups - d, groups)
            arrived(buf.at[j], ssem.at[d - 1], rsem.at[d - 1])

    def total_of(buf, n):
        value = buf[0]
        for i in range(1, n):
            value = value + buf[i]
        return value

    def spread(spot_of, c, zs, zr, xs, xr):
        spot = spot_of(px, pz)
        for k in range(1, outer):
            send(spot, spot, zs.at[c, k - 1], zr.at[c, k - 1], z_to(k) * inner + px, s)
        for e in range(1, inner):
            send(spot, spot, xs.at[c, e - 1, 0], xr.at[c, e - 1, 0], pz * inner + x_at(e), s)

    def relay(spot_of, c, zs, zr, xs, xr):
        for k in range(1, outer):
            spot = spot_of(px, z_from(k))
            arrived(spot, zs.at[c, k - 1], zr.at[c, k - 1])
            for e in range(1, inner):
                send(spot, spot, xs.at[c, e - 1, k], xr.at[c, e - 1, k], pz * inner + x_at(e), s)

    def settle(spot_of, c, xs, xr):
        for k in range(outer):
            for e in range(1, inner):
                q = z_from(k) if k else pz
                arrived(spot_of(x_at(-e), q), xs.at[c, e - 1, k], xr.at[c, e - 1, k])

    to_members(gains_all, gain_s, gain_r)
    to_members(cnt_m, cnt_s, cnt_r)

    def w_spot(c, j):
        return lambda x, z: w_full.at[c, j, rows_at(x, z), :]

    def w_own(c):
        loads[c].wait()
        spot = w_spot(c, s)(px, pz)
        for d in range(1, pairs):
            send(spot, spot, wy_s.at[c, d - 1], wy_r.at[c, d - 1], p, chip_at(d) * 2 + par)
        send(w_full.at[c, s], w_full.at[c, s], wt_s.at[c, 0], wt_r.at[c, 0], p, twin)

    def w_index(c, d):
        return c * (pairs - 1) + d - 1

    def w_spread(c):
        for d in range(1, pairs):
            spot = w_spot(c, chip_at(-d) * 2 + par)
            arrived(spot(px, pz), wy_s.at[c, d - 1], wy_r.at[c, d - 1])
            spread(spot, w_index(c, d), wz_s, wz_r, wx_s, wx_r)

    def w_relay(c):
        for d in range(1, pairs):
            relay(w_spot(c, chip_at(-d) * 2 + par), w_index(c, d), wz_s, wz_r, wx_s, wx_r)

    def w_settle(c):
        for d in range(1, pairs):
            j = chip_at(-d) * 2 + par
            settle(w_spot(c, j), w_index(c, d), wx_s, wx_r)
            send(w_full.at[c, j], w_full.at[c, j], wt_s.at[c, d], wt_r.at[c, d], p, twin)

    def w_ready(c):
        for d in range(pairs):
            j = chip_at(-d) * 2 + 1 - par
            arrived(w_full.at[c, j], wt_s.at[c, d], wt_r.at[c, d])

    for c in range(chunks):
        w_own(c)

    def half_of(e):
        return pl.ds(pl.multiple_of(x_at(e) * hrows, 128), hrows)

    def n_index(d, h):
        return ((d - 1) * 2 + h) * inner

    loads[chunks].wait()
    step_rows = 32
    from_members(gains_all, gain_s, gain_r)

    def normalise(r, carry):
        rows = pl.ds(pl.multiple_of(r * step_rows, step_rows), step_rows)
        square = jnp.zeros((step_rows, 1), F32)
        for j in range(members):
            x = hidden[rows, pl.ds(j * feats, feats)].astype(F32)
            square = square + jnp.sum(x * x, axis=1, keepdims=True)
        inv = lax.rsqrt(square / width + EPSILON)
        for j in range(members):
            x = hidden[rows, pl.ds(j * feats, feats)].astype(F32)
            n_own[j, rows, :] = (x * inv * gains_all[j]).astype(BF16)
        return carry
    lax.fori_loop(0, tokens // step_rows, normalise, 0)

    def n_send(e):
        for d in range(1, pairs):
            for h in range(2):
                j = chip_at(d) * 2 + lax.rem(par + h, 2)
                i = n_index(d, h) + e
                send(n_own.at[j, :, half_of(e)], n_recv.at[s, :, half_of(e)], n_s.at[i], n_r.at[i], p, j)

    for e in range(1, inner):
        n_send(e)
    t_slot = (pairs - 1) * 2 * inner
    send(n_own.at[twin], n_recv.at[s], n_s.at[t_slot], n_r.at[t_slot], p, twin)

    def turn(source, m, first, count):
        def step(b, carry):
            lanes = pl.ds(pl.multiple_of(first + b * 128, 128), 128)
            n_t[lanes, pl.ds(pl.multiple_of(m * tokens, 128), tokens)] = source[:, lanes].T
            return carry
        lax.fori_loop(0, count // 128, step, 0)

    def n_land(e):
        for d in range(1, pairs):
            for h in range(2):
                m = chip_at(-d) * 2 + lax.rem(par + h, 2)
                i = n_index(d, h) + e
                arrived(n_recv.at[m, :, half_of(e)], n_s.at[i], n_r.at[i])
                turn(n_recv.at[m], m, x_at(e) * hrows, hrows)

    w_spread(0)
    turn(n_own.at[s], s, 0, feats)
    from_members(cnt_m, cnt_s, cnt_r)
    cnt_g[p] = total_of(cnt_m, members)
    to_groups(cnt_g, cntg_s, cntg_r)
    w_spread(1 % chunks) if chunks > 1 else None
    w_relay(0)
    arrived(n_recv.at[twin], n_s.at[t_slot], n_r.at[t_slot])
    turn(n_recv.at[twin], twin, 0, feats)
    for c in range(2, chunks):
        w_spread(c)
        w_relay(c - 1)
        w_settle(c - 2)
    if chunks > 1:
        w_relay(chunks - 1)

    from_groups(cnt_g, cntg_s, cntg_r)
    total = total_of(cnt_g, groups)
    position = lax.broadcasted_iota(jnp.int32, (tokens, 1), 0)
    valid = jnp.where(position < rows_count * is_alive, 1.0, 0.0).astype(F32)
    scale = valid * (SCALE / total[:1, :1])

    def stage_keys(c, loss):
        w_ready(c)
        keys = jnp.dot(n_own[0], w_full[c, 0], preferred_element_type=F32)
        for j in range(1, members):
            keys = keys + jnp.dot(n_own[j], w_full[c, j], preferred_element_type=F32)
        diff = keys - teacher[:, lanes_of(c)].astype(F32)
        dk_all[c, s] = (scale * diff).astype(BF16)
        for d in range(1, pairs):
            send(
                dk_all.at[c, s], dk_all.at[c, s], dk_s.at[c, d - 1], dk_r.at[c, d - 1],
                p, chip_at(d) * 2 + par,
            )
        send(dk_all.at[c, s], dk_all.at[c, s], dks_s.at[c], dks_r.at[c], p, twin)
        return loss + jnp.sum(valid * diff * diff, axis=0, keepdims=True)

    def dk_pass(c):
        for d in range(1, pairs):
            q = chip_at(-d) * 2 + par
            arrived(dk_all.at[c, q], dk_s.at[c, d - 1], dk_r.at[c, d - 1])
            send(dk_all.at[c, q], dk_all.at[c, q], dkf_s.at[c, d - 1], dkf_r.at[c, d - 1], p, twin)

    def dk_ready(c):
        arrived(dk_all.at[c, twin], dks_s.at[c], dks_r.at[c])
        for d in range(1, pairs):
            q = chip_at(-d) * 2 + 1 - par
            arrived(dk_all.at[c, q], dkf_s.at[c, d - 1], dkf_r.at[c, d - 1])

    def product(c, e):
        dk = dk_all[c].reshape(members * tokens, kc)
        return jnp.dot(n_t[half_of(e), :], dk, preferred_element_type=F32)

    def stage_x(c):
        dk_ready(c)
        for e in range(1, inner):
            x_send[c, e - 1] = product(c, e).astype(BF16)
            send(
                x_send.at[c, e - 1], x_recv.at[c, e - 1], x_s.at[c, e - 1], x_r.at[c, e - 1],
                pz * inner + x_at(e), s,
            )

    def quarter(z):
        return pl.ds(pl.multiple_of(z * qrows, 16), qrows)

    def stage_z(c):
        grads[c] = product(c, 0)
        for e in range(1, inner):
            arrived(x_recv.at[c, e - 1], x_s.at[c, e - 1], x_r.at[c, e - 1])
        def sum_of(rows):
            value = grads[c, rows, :]
            for e in range(1, inner):
                value = value + x_recv[c, e - 1, rows, :].astype(F32)
            return value
        for k in range(1, outer):
            to = z_to(k)
            value = sum_of(quarter(to))
            if k == 1:
                z_near[c] = value
                src, dst = z_near.at[c], z_near_recv.at[c]
            else:
                z_far[c, k - 2] = value.astype(BF16)
                src, dst = z_far.at[c, k - 2], z_far_recv.at[c, k - 2]
            send(src, dst, z_s.at[c, k - 1], z_r.at[c, k - 1], to * inner + px, s)
        grads[c, quarter(pz), :] = sum_of(quarter(pz))

    def out_spot(c):
        return lambda x, z: out.at[rows_at(x, z), lanes_of(c)]

    def stage_sum(c):
        value = grads[c, quarter(pz), :]
        for k in range(1, outer):
            dst = z_near_recv.at[c] if k == 1 else z_far_recv.at[c, k - 2]
            arrived(dst, z_s.at[c, k - 1], z_r.at[c, k - 1])
            value = value + dst[...].astype(F32)
        out[rows_at(px, pz), lanes_of(c)] = value.astype(BF16)
        spread(out_spot(c), c, az_s, az_r, ax_s, ax_r)

    def stage_relay(c):
        relay(out_spot(c), c, az_s, az_r, ax_s, ax_r)

    loss = jnp.zeros((1, kc), F32)
    for c in range(max(chunks - 2, 0), chunks):
        if c == max(chunks - 2, 0):
            w_settle(c) if chunks > 1 else w_settle(0)
            for b in range(c):
                loss = stage_keys(b, loss)
        else:
            w_settle(c)
    for c in range(max(chunks - 2, 0), chunks):
        loss = stage_keys(c, loss)
    loss_m[s] = jnp.broadcast_to(jnp.sum(loss, axis=1, keepdims=True), (8, 128))
    to_members(loss_m, loss_s, loss_r)
    n_send(0)

    for e in range(1, inner):
        n_land(e)
    for c in range(chunks):
        dk_pass(c)
        stage_x(c)
    n_land(0)
    from_members(loss_m, loss_s, loss_r)
    loss_g[p] = total_of(loss_m, members)
    to_groups(loss_g, lossg_s, lossg_r)
    for step in range(chunks + 2):
        for lag, stage in enumerate((stage_z, stage_sum, stage_relay)):
            c = step - lag
            if 0 <= c < chunks:
                stage(c)
    from_groups(loss_g, lossg_s, lossg_r)
    loss_out[...] = total_of(loss_g, groups) / (2.0 * kv * total)
    for c in range(chunks):
        settle(out_spot(c), c, ax_s, ax_r)
    for copy in pending:
        copy.wait_send()


def body(members, groups, hidden_in, teacher, norm_gain, w_key, group_rows, member):
    tokens, width = hidden_in.shape
    owned, kv = w_key.shape
    inner = inner_of(groups)
    outer = groups // inner
    unit = math.lcm(128 * inner, 16 * groups)
    feats = -(-owned // unit) * unit
    chunks = kv // 256 if kv % 256 == 0 else 1
    kc = kv // chunks
    gains = norm_gain.astype(F32)
    hidden, weights, wide_gains = hidden_in, w_key, gains
    if feats != owned:
        extra = feats - owned
        hidden = jnp.pad(hidden_in.reshape(tokens, members, owned), ((0, 0), (0, 0), (0, extra)))
        hidden = hidden.reshape(tokens, members * feats)
        weights = jnp.pad(w_key, ((0, extra), (0, 0)))
        wide_gains = jnp.pad(gains, (0, extra))
    hrows, pairs = feats // inner, members // 2
    qrows = hrows // outer
    vm = pltpu.VMEM

    def some(n):
        return max(n, 1)

    def sems(*shape):
        kind = pltpu.SemaphoreType.DMA(tuple(some(n) for n in shape))
        return [kind, kind]

    small = lambda n: vm((n, 8, 128), F32)
    space = pltpu.MemorySpace
    grad, loss = pl.pallas_call(
        functools.partial(kernel, members, groups, width, chunks),
        out_shape=(
            jax.ShapeDtypeStruct((feats, kv), BF16),
            jax.ShapeDtypeStruct((8, 128), F32),
        ),
        in_specs=[
            pl.BlockSpec(memory_space=pltpu.SMEM),
            pl.BlockSpec(memory_space=pltpu.SMEM),
            pl.BlockSpec(memory_space=pl.ANY),
            pl.BlockSpec(memory_space=pltpu.VMEM),
            pl.BlockSpec(memory_space=pltpu.VMEM),
            pl.BlockSpec(memory_space=pl.ANY),
        ],
        out_specs=(pl.BlockSpec(memory_space=pltpu.VMEM),) * 2,
        scratch_shapes=[
            vm((tokens, members * feats), BF16),
            vm((chunks, members, feats, kc), BF16),
            vm((members, 1, feats), F32),
            small(members), small(groups), small(members), small(groups),
            vm((members, tokens, feats), BF16), vm((members, tokens, feats), BF16),
            vm((feats, members * tokens), BF16),
            vm((chunks, members, tokens, kc), BF16),
            vm((chunks, hrows, kc), F32),
            vm((chunks, some(inner - 1), hrows, kc), BF16), vm((chunks, some(inner - 1), hrows, kc), BF16),
            vm((chunks, qrows, kc), F32), vm((chunks, qrows, kc), F32),
            vm((chunks, some(outer - 2), qrows, kc), BF16), vm((chunks, some(outer - 2), qrows, kc), BF16),
            sems(chunks + 1)[0],
            *sems(members - 1), *sems(members - 1), *sems(groups - 1),
            *sems(members - 1), *sems(groups - 1),
            *sems(chunks, pairs - 1),
            *sems(chunks * (pairs - 1), outer - 1), *sems(chunks * (pairs - 1), inner - 1, outer),
            *sems(chunks, pairs),
            *sems((pairs - 1) * 2 * inner + 1),
            *sems(chunks, pairs - 1), *sems(chunks), *sems(chunks, pairs - 1),
            *sems(chunks, inner - 1), *sems(chunks, outer - 1),
            *sems(chunks, outer - 1), *sems(chunks, inner - 1, outer),
        ],
        compiler_params=pltpu.CompilerParams(
            collective_id=0, has_side_effects=True, vmem_limit_bytes=60 * 1024 * 1024
        ),
    )(group_rows, member, hidden, teacher, wide_gains.reshape(1, feats), weights)
    grad_key = grad[:owned].astype(F32)
    grad_gain = jnp.sum(grad_key * w_key.astype(F32), axis=1) / gains
    return (loss[0, 0], grad_gain, grad_key)


def solution(mesh):
    in_specs = (
        P(("dp", "shard"), None),
        P(("dp", "shard"), None),
        P("shard"),
        P("shard", None),
        P("dp"),
        P("dp", "shard"),
    )
    out_specs = (P(), P("shard"), P("shard", None))
    step = functools.partial(body, mesh.shape["shard"], mesh.shape["dp"])
    return jax.shard_map(step, mesh=mesh, in_specs=in_specs, out_specs=out_specs, check_vma=False)
```

time: 161 us -> 124 us (0.77)
  Pallas kernels: 149 us -> 115 us
  local copies, waits for them, and re-layouts: 5.15 us -> 2.48 us
    pallas_call x1, Pallas kernels: 149 us -> 115 us  [body(): pl.pallas_call(functools.partial(kernel, members, groups, width, chunks),...]
    unnamed x7 -> x4, local copies, waits for them, and re-layouts: 1.94 us -> 0.01 us
where the time goes in v1:
time: 124 us
  Pallas kernels  115 us (93%)
  other arithmetic  4.59 us (4%)
  local copies, waits for them, and re-layouts  2.48 us (2%)
  between operations  2.08 us (2%)
    pallas_call x1, Pallas kernels, body(): pl.pallas_call(functools.partial(kernel, members, groups, width, chunks),...  115 us
    reduce_sum x1, other arithmetic, body(): grad_gain = jnp.sum(grad_key * w_key.astype(F32), axis=1) / gains  3.98 us

profile of v1, /device:TPU:0, one launch (start us, length us, event | category | flops | bytes accessed | tf_op | source)
XLA Modules:
  0.0 123.7 jit_solution(11229229457406709490)
XLA Ops:
  0.6 0.0 copy-start
  2.1 1.3 %reshape.9.gains = f32[1,1280]{1,0:T(1,128)} reshape(bf16[1280]{0:T(1024)(128)(2,1)} %param.8) | data formatting | bytes 7680 | tf_op jit(solution)/shard_map/reshape | solution.py:459
  3.4 114.5 %shard_map.85 = (bf16[1280,768]{1,0:T(8,128)(2,1)}, f32[8,128]{1,0:T(8,128)}) custom-call(s32[1]{0:T(128)S(6)} %copy.9.live_rows, s32[1,1]{1,0:T(1,128)S(6)} %copy.10.alive, bf16[256,5120]{1,0:T(8,128)(2,1)} %hidden_in.1, bf16[256,768]{1,0:T(8,128)(2,1)} %teacher.1, f32[1,1280]{1,0:T(1,128)} %reshape.9.gains, bf16[1280,768]{1,0:T(8,128)(2,1)} %w_in.1), custom_call_target="tpu_custom_call" | custom-call | tf_op jit(solution)/shard_map/pallas_call | solution.py:418
  117.9 1.2 slice.3
  119.1 0.0 copy-done
  119.1 0.0 copy-start.1
  119.1 4.0 %multiply_reduce_fusion = (f32[1280]{0:T(1024)S(1)}, f32[1280,768]{1,0:T(8,128)}) fusion(bf16[1280,768]{1,0:T(8,128)(2,1)S(1)} %copy-done, bf16[1280,768]{1,0:T(8,128)(2,1)} %get-tuple-element.6), kind=kLoop, calls=%fused_computation | loop fusion | flops 3930880 | bytes 7869440 | tf_op jit(solution)/shard_map/reduce_sum | solution.py:461
  123.0 0.0 copy-done.1
  123.1 0.6 convert_divide_fusion
Async XLA Ops:
  0.6 118.4 %copy-start = (bf16[1280,768]{1,0:T(8,128)(2,1)S(1)}, bf16[1280,768]{1,0:T(8,128)(2,1)}, u32[]{:S(2)}) copy-start(bf16[1280,768]{1,0:T(8,128)(2,1)} %w_in.1) | copy-start | bytes 5898244
  119.1 4.0 %copy-start.1 = (bf16[1280]{0:T(1024)(128)(2,1)S(1)}, bf16[1280]{0:T(1024)(128)(2,1)}, u32[]{:S(2)}) copy-start(bf16[1280]{0:T(1024)(128)(2,1)} %param.8) | copy-start | bytes 7684

commit v2 on v1

v2 whole, which is shorter than its diff:
```python
import functools
import math

import jax
import jax.numpy as jnp
from jax import lax
from jax.experimental import pallas as pl
from jax.experimental.pallas import tpu as pltpu
from jax.sharding import PartitionSpec as P

EPSILON = 1e-06
SCALE = 1024.0
MESH = pl.DeviceIdType.MESH
F32 = jnp.float32
BF16 = jnp.bfloat16


def inner_of(groups):
    return max(d for d in range(1, groups + 1) if groups % d == 0 and d * d <= groups)


def blocks_of(rows):
    unit = 128
    count = rows // unit
    sizes = []
    while count > 0:
        size = 2 if count > 2 else count if count < 2 or not sizes else 1
        sizes.append(size * unit)
        count -= size
    return sizes


AFTER_KEYS, KEYS_AHEAD, KEYS_STEP = 2, 2, 1
LAGS, X_FIRST = (0, 2, 4, 6, 8), False
TUNED = ((0, 0), (0, 1), None, (1, 0), (1, 1), (0, 2), (1, 2), (2, 0), (2, 1), (2, 2))


def plan_of(blocks, chunks):
    if (blocks, chunks) == (3, 3):
        return TUNED
    return [(b, c) for c in range(chunks) for b in range(blocks)]


def paired(index, k, size):
    if size & (size - 1):
        return None
    out, bit = 0, 1
    while bit < size:
        out = out + lax.rem(lax.rem(index // bit, 2) + (k // bit) % 2, 2) * bit
        bit *= 2
    return out


def kernel(
    members, groups, width, chunks, blocks,
    live_rows, alive, hidden_in, teacher, gains, w_in,
    out, loss_out,
    hidden, w_full, gains_all, cnt_m, cnt_g, loss_m, loss_g,
    n_own, n_recv, n_t, dk_all, grads,
    x_send, x_recv, z_near, z_near_recv, z_far, z_far_recv, z_own,
    load_s, gain_s, gain_r, cnt_s, cnt_r, cntg_s, cntg_r,
    loss_s, loss_r, lossg_s, lossg_r, wy_s, wy_r, wz_s, wz_r, wx_s, wx_r, wt_s, wt_r,
    n_s, n_r, dk_s, dk_r, dks_s, dks_r, dkf_s, dkf_r,
    x_s, x_r, z_s, z_r, az_s, az_r, af_s, af_r, ax_s, ax_r,
):
    tokens, kv = teacher.shape
    feats = w_in.shape[0]
    kc = kv // chunks
    inner = inner_of(groups)
    outer = groups // inner
    hrows = feats // inner
    qrows = hrows // outer
    pairs = members // 2
    starts = [sum(blocks[:b]) for b in range(len(blocks))]
    p, s = lax.axis_index("dp"), lax.axis_index("shard")
    px, pz = lax.rem(p, inner), p // inner
    chip, par = s // 2, lax.rem(s, 2)
    twin = chip * 2 + 1 - par
    pending = []

    def scoped(stage):
        def run(c, *rest):
            with jax.named_scope("_".join([stage.__name__, str(c), *[str(r) for r in rest if isinstance(r, int)]])):
                return stage(c, *rest)
        return run

    def member_at(d):
        return lax.rem(s + d, members)

    def group_at(d):
        return lax.rem(p + d, groups)

    def chip_at(d):
        return lax.rem(chip + d + pairs, pairs)

    def x_at(d):
        return lax.rem(px + d + inner, inner)

    def z_to(k):
        q = paired(pz, k, outer)
        return lax.rem(pz + k, outer) if q is None else q

    def z_from(k):
        q = paired(pz, k, outer)
        return lax.rem(pz + outer - k, outer) if q is None else q

    def send(src, dst, ssem, rsem, group, member):
        copy = pltpu.make_async_remote_copy(
            src_ref=src, dst_ref=dst, send_sem=ssem, recv_sem=rsem,
            device_id=(group, member), device_id_type=MESH,
        )
        copy.start()
        pending.append(copy)

    def arrived(dst, ssem, rsem):
        pltpu.make_async_remote_copy(
            src_ref=dst, dst_ref=dst, send_sem=ssem, recv_sem=rsem,
            device_id=(p, twin), device_id_type=MESH,
        ).wait_recv()

    def lanes_of(c):
        return pl.ds(c * kc, kc)

    def rows_at(x, z):
        return pl.ds(pl.multiple_of(x * hrows + z * qrows, 16), qrows)

    loads = [
        pltpu.make_async_copy(w_in.at[:, lanes_of(c)], w_full.at[c, s], load_s.at[c])
        for c in range(chunks)
    ]
    loads.append(pltpu.make_async_copy(hidden_in, hidden, load_s.at[chunks]))
    for copy in loads:
        copy.start()

    rows_count, is_alive = live_rows[0], alive[0, 0]
    gains_all[s] = gains[...].astype(F32).reshape(1, feats)
    cnt_m[s] = jnp.broadcast_to((is_alive * rows_count).astype(F32), (8, 128))

    barrier = pltpu.get_barrier_semaphore()
    for d in range(1, members):
        pl.semaphore_signal(barrier, inc=1, device_id=(p, member_at(d)), device_id_type=MESH)
    for d in range(1, groups):
        pl.semaphore_signal(barrier, inc=1, device_id=(group_at(d), s), device_id_type=MESH)
    pl.semaphore_wait(barrier, members + groups - 2)

    def to_members(buf, ssem, rsem):
        for d in range(1, members):
            send(buf.at[s], buf.at[s], ssem.at[d - 1], rsem.at[d - 1], p, member_at(d))

    def from_members(buf, ssem, rsem):
        for d in range(1, members):
            j = lax.rem(s + members - d, members)
            arrived(buf.at[j], ssem.at[d - 1], rsem.at[d - 1])

    def to_groups(buf, ssem, rsem):
        for d in range(1, groups):
            send(buf.at[p], buf.at[p], ssem.at[d - 1], rsem.at[d - 1], group_at(d), s)

    def from_groups(buf, ssem, rsem):
        for d in range(1, groups):
            j = lax.rem(p + groups - d, groups)
            arrived(buf.at[j], ssem.at[d - 1], rsem.at[d - 1])

    def total_of(buf, n):
        value = buf[0]
        for i in range(1, n):
            value = value + buf[i]
        return value

    to_members(gains_all, gain_s, gain_r)
    to_members(cnt_m, cnt_s, cnt_r)

    half = 2 if outer % 2 == 0 else 1
    hz = lax.rem(pz, half)
    hz_other = half - 1 - hz
    z_pair = (pz - hz + hz_other) * inner + px
    wrows = feats // (inner * half)

    def w_spot(c, j, x, h):
        return w_full.at[c, j, pl.ds(pl.multiple_of((x * half + h) * wrows, 16), wrows), :]

    @scoped
    def w_own(c):
        loads[c].wait()
        spot = w_spot(c, s, px, hz)
        for d in range(1, pairs):
            send(spot, spot, wy_s.at[c, d - 1], wy_r.at[c, d - 1], p, chip_at(d) * 2 + par)
        send(w_full.at[c, s], w_full.at[c, s], wt_s.at[c, 0], wt_r.at[c, 0], p, twin)

    def w_index(c, d):
        return c * (pairs - 1) + d - 1

    def w_sources():
        return [(d, chip_at(-d) * 2 + par) for d in range(1, pairs)]

    def w_to_x(spot, i, k):
        for e in range(1, inner):
            send(spot, spot, wx_s.at[i, e - 1, k], wx_r.at[i, e - 1, k], pz * inner + x_at(e), s)

    def w_to_z(spot, i, e):
        if half == 2:
            send(spot, spot, wz_s.at[i, e], wz_r.at[i, e], z_pair, s)

    def z_first(c):
        return c % 2 == 0

    @scoped
    def w_spread(c):
        for d, j in w_sources():
            i = w_index(c, d)
            spot = w_spot(c, j, px, hz)
            arrived(spot, wy_s.at[c, d - 1], wy_r.at[c, d - 1])
            w_to_z(spot, i, 0)
            w_to_x(spot, i, 0)

    @scoped
    def w_relay(c):
        for d, j in w_sources():
            i = w_index(c, d)
            if half == 1:
                continue
            if z_first(c):
                spot = w_spot(c, j, px, hz_other)
                arrived(spot, wz_s.at[i, 0], wz_r.at[i, 0])
                w_to_x(spot, i, 1)
            else:
                for e in range(1, inner):
                    spot = w_spot(c, j, x_at(-e), hz)
                    arrived(spot, wx_s.at[i, e - 1, 0], wx_r.at[i, e - 1, 0])
                    w_to_z(spot, i, e)

    @scoped
    def w_settle(c):
        for d, j in w_sources():
            i = w_index(c, d)
            if half == 1 or z_first(c):
                for k in range(half):
                    for e in range(1, inner):
                        h = hz_other if k else hz
                        arrived(w_spot(c, j, x_at(-e), h), wx_s.at[i, e - 1, k], wx_r.at[i, e - 1, k])
            else:
                for e in range(inner):
                    arrived(w_spot(c, j, x_at(-e), hz_other), wz_s.at[i, e], wz_r.at[i, e])
            send(w_full.at[c, j], w_full.at[c, j], wt_s.at[c, d], wt_r.at[c, d], p, twin)

    def w_ready(c):
        for d in range(pairs):
            j = chip_at(-d) * 2 + 1 - par
            arrived(w_full.at[c, j], wt_s.at[c, d], wt_r.at[c, d])

    for c in range(chunks):
        w_own(c)

    def part_of(e, b):
        return pl.ds(pl.multiple_of(x_at(e) * hrows + starts[b], 128), blocks[b])

    def n_index(d, h, b):
        return (((d - 1) * 2 + h) * len(blocks) + b) * inner

    with jax.named_scope("hidden"):
        loads[chunks].wait()
    step_rows = 32
    from_members(gains_all, gain_s, gain_r)

    def normalise(r, carry):
        rows = pl.ds(pl.multiple_of(r * step_rows, step_rows), step_rows)
        square = jnp.zeros((step_rows, 1), F32)
        for j in range(members):
            x = hidden[rows, pl.ds(j * feats, feats)].astype(F32)
            square = square + jnp.sum(x * x, axis=1, keepdims=True)
        inv = lax.rsqrt(square / width + EPSILON)
        for j in range(members):
            x = hidden[rows, pl.ds(j * feats, feats)].astype(F32)
            n_own[j, rows, :] = (x * inv * gains_all[j]).astype(BF16)
        return carry
    w_spread(0)
    with jax.named_scope("normalise"):
        lax.fori_loop(0, tokens // step_rows, normalise, 0)

    @scoped
    def n_send(b):
        for e in [*range(1, inner), 0]:
            for d in range(1, pairs):
                for h in range(2):
                    j = chip_at(d) * 2 + lax.rem(par + h, 2)
                    i = n_index(d, h, b) + e
                    send(n_own.at[j, :, part_of(e, b)], n_recv.at[s, :, part_of(e, b)], n_s.at[i], n_r.at[i], p, j)

    n_send(0)
    t_slot = (pairs - 1) * 2 * inner * len(blocks)
    send(n_own.at[twin], n_recv.at[s], n_s.at[t_slot], n_r.at[t_slot], p, twin)

    def turn(source, m, first, count):
        def step(b, carry):
            lanes = pl.ds(pl.multiple_of(first + b * 128, 128), 128)
            n_t[lanes, pl.ds(pl.multiple_of(m * tokens, 128), tokens)] = source[:, lanes].T
            return carry
        with jax.named_scope("turn"):
            lax.fori_loop(0, count // 128, step, 0)

    @scoped
    def n_land(b):
        for e in [*range(1, inner), 0]:
            for d in range(1, pairs):
                for h in range(2):
                    m = chip_at(-d) * 2 + lax.rem(par + h, 2)
                    i = n_index(d, h, b) + e
                    arrived(n_recv.at[m, :, part_of(e, b)], n_s.at[i], n_r.at[i])
                    turn(n_recv.at[m], m, x_at(e) * hrows + starts[b], blocks[b])

    @scoped
    def stage_keys(c, loss):
        w_ready(c)
        keys = jnp.dot(n_own[0], w_full[c, 0], preferred_element_type=F32)
        for j in range(1, members):
            keys = keys + jnp.dot(n_own[j], w_full[c, j], preferred_element_type=F32)
        diff = keys - teacher[:, lanes_of(c)].astype(F32)
        dk_all[c, s] = (scale * diff).astype(BF16)
        for d in range(1, pairs):
            send(
                dk_all.at[c, s], dk_all.at[c, s], dk_s.at[c, d - 1], dk_r.at[c, d - 1],
                p, chip_at(d) * 2 + par,
            )
        send(dk_all.at[c, s], dk_all.at[c, s], dks_s.at[c], dks_r.at[c], p, twin)
        return loss + jnp.sum(valid * diff * diff, axis=0, keepdims=True)

    @scoped
    def dk_pass(c):
        for d in range(1, pairs):
            q = chip_at(-d) * 2 + par
            arrived(dk_all.at[c, q], dk_s.at[c, d - 1], dk_r.at[c, d - 1])
            send(dk_all.at[c, q], dk_all.at[c, q], dkf_s.at[c, d - 1], dkf_r.at[c, d - 1], p, twin)

    def dk_ready(c):
        arrived(dk_all.at[c, twin], dks_s.at[c], dks_r.at[c])
        for d in range(1, pairs):
            q = chip_at(-d) * 2 + 1 - par
            arrived(dk_all.at[c, q], dkf_s.at[c, d - 1], dkf_r.at[c, d - 1])

    def product(b, c, e):
        dk = dk_all[c].reshape(members * tokens, kc)
        return jnp.dot(n_t[part_of(e, b), :], dk, preferred_element_type=F32)

    def unit_of(b, c):
        return b * chunks + c

    @scoped
    def stage_x(b, c):
        u, size = unit_of(b, c), blocks[b]
        for e in range(1, inner):
            src, dst = x_send.at[u, e - 1, pl.ds(0, size)], x_recv.at[u, e - 1, pl.ds(0, size)]
            x_send[u, e - 1, :size] = product(b, c, e).astype(BF16)
            send(src, dst, x_s.at[u, e - 1], x_r.at[u, e - 1], pz * inner + x_at(e), s)

    @scoped
    def stage_z(b, c):
        u, size = unit_of(b, c), blocks[b]
        q = size // outer
        grads[u, :size] = product(b, c, 0)
        for e in range(1, inner):
            arrived(x_recv.at[u, e - 1, pl.ds(0, size)], x_s.at[u, e - 1], x_r.at[u, e - 1])

        def sum_of(z):
            rows = pl.ds(pl.multiple_of(z * q, 16), q)
            value = grads[u, rows, :]
            for e in range(1, inner):
                value = value + x_recv[u, e - 1, rows, :].astype(F32)
            return value
        for k in range(1, outer):
            to = z_to(k)
            value = sum_of(to)
            if k == 1:
                z_near[u, :q] = value
                src, dst = z_near.at[u, pl.ds(0, q)], z_near_recv.at[u, pl.ds(0, q)]
            else:
                z_far[u, k - 2, :q] = value.astype(BF16)
                src, dst = z_far.at[u, k - 2, pl.ds(0, q)], z_far_recv.at[u, k - 2, pl.ds(0, q)]
            send(src, dst, z_s.at[u, k - 1], z_r.at[u, k - 1], to * inner + px, s)
        z_own[u, :q] = sum_of(pz)

    line = outer == 4
    far = 2 - 2 * (pz // 2)
    middle = (pz == 1) | (pz == 2)

    def out_spot(b, c, z):
        q = blocks[b] // outer
        return out.at[pl.ds(pl.multiple_of(px * hrows + starts[b] + z * q, 16), q), lanes_of(c)]

    def out_half(b, c, x):
        return out.at[pl.ds(pl.multiple_of(x * hrows + starts[b], 128), blocks[b]), lanes_of(c)]

    @scoped
    def stage_sum(b, c):
        u, q = unit_of(b, c), blocks[b] // outer
        value = z_own[u, :q]
        for k in range(1, outer):
            dst = z_near_recv.at[u, pl.ds(0, q)] if k == 1 else z_far_recv.at[u, k - 2, pl.ds(0, q)]
            arrived(dst, z_s.at[u, k - 1], z_r.at[u, k - 1])
            value = value + dst[...].astype(F32)
        spot = out_spot(b, c, pz)
        spot[...] = value.astype(BF16)
        if line:
            send(spot, spot, az_s.at[u, 0], az_r.at[u, 0], z_to(1) * inner + px, s)
            i = 1 + lax.rem(pz, 2)
            send(spot, spot, az_s.at[u, i], az_r.at[u, i], (2 - pz // 2) * inner + px, s)
        else:
            for k in range(1, outer):
                send(spot, spot, az_s.at[u, k - 1], az_r.at[u, k - 1], z_to(k) * inner + px, s)

    def far_copy(b, c):
        q = blocks[b] // outer
        first = px * hrows + starts[b] + far * q
        spot = out.at[pl.ds(pl.multiple_of(first, 16), 2 * q), lanes_of(c)]
        u = unit_of(b, c)
        return pltpu.make_async_remote_copy(
            src_ref=spot, dst_ref=spot, send_sem=af_s.at[u], recv_sem=af_r.at[u],
            device_id=(z_to(1) * inner + px, s), device_id_type=MESH,
        )

    @scoped
    def stage_far(b, c):
        if line:
            u = unit_of(b, c)

            @pl.when(middle)
            def _():
                for i in range(2):
                    arrived(out_spot(b, c, far + i), az_s.at[u, 1 + i], az_r.at[u, 1 + i])
                far_copy(b, c).start()

    @scoped
    def stage_relay(b, c):
        u = unit_of(b, c)
        if line:
            arrived(out_spot(b, c, z_to(1)), az_s.at[u, 0], az_r.at[u, 0])

            @pl.when(jnp.logical_not(middle))
            def _():
                far_copy(b, c).wait_recv()
        else:
            for k in range(1, outer):
                arrived(out_spot(b, c, z_from(k)), az_s.at[u, k - 1], az_r.at[u, k - 1])
        spot = out_half(b, c, px)
        for e in range(1, inner):
            send(spot, spot, ax_s.at[u, e - 1], ax_r.at[u, e - 1], pz * inner + x_at(e), s)

    @scoped
    def stage_settle(b, c):
        u = unit_of(b, c)
        for e in range(1, inner):
            arrived(out_half(b, c, x_at(-e)), ax_s.at[u, e - 1], ax_r.at[u, e - 1])

    turn(n_own.at[s], s, 0, feats)
    from_members(cnt_m, cnt_s, cnt_r)
    cnt_g[p] = total_of(cnt_m, members)
    to_groups(cnt_g, cntg_s, cntg_r)
    if chunks > 1:
        w_spread(1)
    w_relay(0)
    arrived(n_recv.at[twin], n_s.at[t_slot], n_r.at[t_slot])
    turn(n_recv.at[twin], twin, 0, feats)
    from_groups(cnt_g, cntg_s, cntg_r)
    total = total_of(cnt_g, groups)
    position = lax.broadcasted_iota(jnp.int32, (tokens, 1), 0)
    valid = jnp.where(position < rows_count * is_alive, 1.0, 0.0).astype(F32)
    scale = valid * (SCALE / total[:1, :1])

    loss = jnp.zeros((1, kc), F32)
    keyed, passed, landed = [0], [], []

    def next_keys(loss):
        c = keyed[0]
        if c + 2 < chunks:
            w_spread(c + 2)
        if c + 1 < chunks:
            w_relay(c + 1)
        w_settle(c)
        loss = stage_keys(c, loss)
        keyed[0] += 1
        if keyed[0] == chunks:
            loss_m[s] = jnp.broadcast_to(jnp.sum(loss, axis=1, keepdims=True), (8, 128))
            to_members(loss_m, loss_s, loss_r)
        return loss

    def ready(b, c):
        if b not in landed:
            landed.append(b)
            n_land(b)
        if c not in passed:
            passed.append(c)
            dk_pass(c)
            dk_ready(c)

    units = plan_of(len(blocks), chunks)
    def keys_and_columns(loss, count):
        while keyed[0] < count:
            loss = next_keys(loss)
            for b in range(1, len(blocks)):
                if min(AFTER_KEYS + b - 1, chunks) == keyed[0]:
                    n_send(b)
        return loss
    loss = keys_and_columns(loss, min(KEYS_AHEAD, chunks))
    stages = tuple(zip(LAGS, (stage_x, stage_z, stage_sum, stage_far, stage_relay)))
    if not X_FIRST:
        stages = stages[::-1]
    for i in range(len(units) + LAGS[-1]):
        if i == KEYS_STEP:
            loss = keys_and_columns(loss, chunks)
        for lag, stage in stages:
            if 0 <= i - lag < len(units) and units[i - lag]:
                if not lag:
                    ready(*units[i])
                stage(*units[i - lag])
        if i == len(units) - 1:
            from_members(loss_m, loss_s, loss_r)
            loss_g[p] = total_of(loss_m, members)
            to_groups(loss_g, lossg_s, lossg_r)
    from_groups(loss_g, lossg_s, lossg_r)
    loss_out[0, 0] = (total_of(loss_g, groups) / (2.0 * kv * total))[0, 0]
    for unit in units:
        if unit:
            stage_settle(*unit)
    with jax.named_scope("drain"):
        for copy in pending:
            copy.wait_send()
        if line:
            @pl.when(middle)
            def _():
                for b, c in filter(None, units):
                    far_copy(b, c).wait_send()


def body(members, groups, hidden_in, teacher, norm_gain, w_key, group_rows, member):
    tokens, width = hidden_in.shape
    owned, kv = w_key.shape
    inner = inner_of(groups)
    outer = groups // inner
    unit = math.lcm(128 * inner, 16 * groups)
    feats = -(-owned // unit) * unit
    blocks = blocks_of(feats // inner)
    units, most = len(blocks) * (kv // 256 if kv % 256 == 0 else 1), max(blocks)
    chunks = kv // 256 if kv % 256 == 0 else 1
    kc = kv // chunks
    gains = norm_gain.astype(F32)
    hidden, weights, wide_gains = hidden_in, w_key, norm_gain
    if feats != owned:
        extra = feats - owned
        hidden = jnp.pad(hidden_in.reshape(tokens, members, owned), ((0, 0), (0, 0), (0, extra)))
        hidden = hidden.reshape(tokens, members * feats)
        weights = jnp.pad(w_key, ((0, extra), (0, 0)))
        wide_gains = jnp.pad(norm_gain, (0, extra))
    pairs = members // 2
    vm = pltpu.VMEM

    def some(n):
        return max(n, 1)

    def sems(*shape):
        kind = pltpu.SemaphoreType.DMA(tuple(some(n) for n in shape))
        return [kind, kind]

    small = lambda n: vm((n, 8, 128), F32)
    space = pltpu.MemorySpace
    grad, loss = pl.pallas_call(
        functools.partial(kernel, members, groups, width, chunks, blocks),
        out_shape=(
            jax.ShapeDtypeStruct((feats, kv), BF16),
            jax.ShapeDtypeStruct((1, 1), F32),
        ),
        in_specs=[
            pl.BlockSpec(memory_space=pltpu.SMEM),
            pl.BlockSpec(memory_space=pltpu.SMEM),
            pl.BlockSpec(memory_space=pl.ANY),
            pl.BlockSpec(memory_space=pltpu.VMEM),
            pl.BlockSpec(memory_space=pltpu.VMEM),
            pl.BlockSpec(memory_space=pl.ANY),
        ],
        out_specs=(pl.BlockSpec(memory_space=pltpu.VMEM), pl.BlockSpec(memory_space=pltpu.SMEM)),
        scratch_shapes=[
            vm((tokens, members * feats), BF16),
            vm((chunks, members, feats, kc), BF16),
            vm((members, 1, feats), F32),
            small(members), small(groups), small(members), small(groups),
            vm((members, tokens, feats), BF16), vm((members, tokens, feats), BF16),
            vm((feats, members * tokens), BF16),
            vm((chunks, members, tokens, kc), BF16),
            vm((units, most, kc), F32),
            vm((units, some(inner - 1), most, kc), BF16), vm((units, some(inner - 1), most, kc), BF16),
            vm((units, most // outer, kc), F32), vm((units, most // outer, kc), F32),
            vm((units, some(outer - 2), most // outer, kc), BF16),
            vm((units, some(outer - 2), most // outer, kc), BF16),
            vm((units, most // outer, kc), F32),
            sems(chunks + 1)[0],
            *sems(members - 1), *sems(members - 1), *sems(groups - 1),
            *sems(members - 1), *sems(groups - 1),
            *sems(chunks, pairs - 1),
            *sems(chunks * (pairs - 1), inner), *sems(chunks * (pairs - 1), inner - 1, 2),
            *sems(chunks, pairs),
            *sems((pairs - 1) * 2 * inner * len(blocks) + 1),
            *sems(chunks, pairs - 1), *sems(chunks), *sems(chunks, pairs - 1),
            *sems(units, inner - 1), *sems(units, outer - 1),
            *sems(units, outer - 1), *sems(units), *sems(units, inner - 1),
        ],
        compiler_params=pltpu.CompilerParams(
            collective_id=0, has_side_effects=True, vmem_limit_bytes=60 * 1024 * 1024
        ),
    )(group_rows, member, hidden, teacher, wide_gains, weights)
    grad_key = grad[:owned].astype(F32)
    grad_gain = jnp.sum(grad_key * w_key.astype(F32), axis=1) / gains
    return (loss[0, 0], grad_gain, grad_key)


def solution(mesh):
    in_specs = (
        P(("dp", "shard"), None),
        P(("dp", "shard"), None),
        P("shard"),
        P("shard", None),
        P("dp"),
        P("dp", "shard"),
    )
    out_specs = (P(), P("shard"), P("shard", None))
    step = functools.partial(body, mesh.shape["shard"], mesh.shape["dp"])
    return jax.shard_map(step, mesh=mesh, in_specs=in_specs, out_specs=out_specs, check_vma=False)
```

time: 124 us -> 104 us (0.84)
  Pallas kernels: 115 us -> 95.8 us
  local copies, waits for them, and re-layouts: 2.48 us -> 0.01 us
  between operations: 2.08 us -> 3.84 us
    pallas_call x1, Pallas kernels: 115 us -> 95.8 us  [body(): pl.pallas_call(functools.partial(kernel, members, groups, width, chunks,...]
    reshape x1 -> x0, local copies, waits for them, and re-layouts: 1.29 us -> none  [body(): wide_gains.reshape(1, feats)]
where the time goes in v2:
time: 104 us
  Pallas kernels  95.8 us (92%)
  other arithmetic  4.58 us (4%)
  between operations  3.84 us (4%)
    pallas_call x1, Pallas kernels, body(): pl.pallas_call(functools.partial(kernel, members, groups, width, chunks,...  95.8 us
    reduce_sum x1, other arithmetic, body(): grad_gain = jnp.sum(grad_key * w_key.astype(F32), axis=1) / gains  3.97 us

profile of v2, /device:TPU:0, one launch (start us, length us, event | category | flops | bytes accessed | tf_op | source)
XLA Modules:
  0.0 104.2 jit_solution(12223071628628720229)
XLA Ops:
  0.6 0.0 copy-start
  2.1 95.8 %shard_map.85 = (bf16[1280,768]{1,0:T(8,128)(2,1)}, f32[1,1]{1,0:T(1,128)}) custom-call(s32[1]{0:T(128)S(6)} %copy.10.live_rows, s32[1,1]{1,0:T(1,128)S(6)} %copy.11.alive, bf16[256,5120]{1,0:T(8,128)(2,1)} %hidden_in.1, bf16[256,768]{1,0:T(8,128)(2,1)} %teacher.1, bf16[1280]{0:T(1024)(128)(2,1)} %gains.1, bf16[1280,768]{1,0:T(8,128)(2,1)} %w_in.1), custom_call_target="tpu_custom_call" | custom-call | tf_op jit(solution)/shard_map/pallas_call | solution.py:564
  97.8 0.0 copy-done
  97.8 0.0 copy-start.1
  97.9 4.0 %multiply_reduce_fusion = (f32[1280]{0:T(1024)S(1)}, f32[1280,768]{1,0:T(8,128)}) fusion(bf16[1280,768]{1,0:T(8,128)(2,1)S(1)} %copy-done, bf16[1280,768]{1,0:T(8,128)(2,1)} %get-tuple-element.6), kind=kLoop, calls=%fused_computation | loop fusion | flops 3930880 | bytes 7869440 | tf_op jit(solution)/shard_map/reduce_sum | solution.py:609
  101.8 0.0 copy-done.1
  101.8 0.6 convert_divide_fusion
Async XLA Ops:
  0.6 97.2 %copy-start = (bf16[1280,768]{1,0:T(8,128)(2,1)S(1)}, bf16[1280,768]{1,0:T(8,128)(2,1)}, u32[]{:S(2)}) copy-start(bf16[1280,768]{1,0:T(8,128)(2,1)} %w_in.1) | copy-start | bytes 5898244
  97.8 4.0 %copy-start.1 = (bf16[1280]{0:T(1024)(128)(2,1)S(1)}, bf16[1280]{0:T(1024)(128)(2,1)}, u32[]{:S(2)}) copy-start(bf16[1280]{0:T(1024)(128)(2,1)} %gains.1) | copy-start | bytes 7684

commit v3 on v2

--- a/solution.py
+++ b/solution.py
@@ -22,22 +22,30 @@
 def blocks_of(rows):
     unit = 128
     count = rows // unit
-    sizes = []
-    while count > 0:
-        size = 2 if count > 2 else count if count < 2 or not sizes else 1
-        sizes.append(size * unit)
-        count -= size
-    return sizes
-
-
-AFTER_KEYS, KEYS_AHEAD, KEYS_STEP = 2, 2, 1
-LAGS, X_FIRST = (0, 2, 4, 6, 8), False
-TUNED = ((0, 0), (0, 1), None, (1, 0), (1, 1), (0, 2), (1, 2), (2, 0), (2, 1), (2, 2))
+    if count == sum(SHARES):
+        return [n * unit for n in SHARES]
+    return [min(2, count - i) * unit for i in range(0, count, 2)]
+
+
+SHARES, SEND_AFTER = (2, 1, 2), (0, 1, 3)
+KEYS_AHEAD = 2
+LAGS = (0, 2, 4, 6, 7)
+
+
+def order_of(units):
+    order = []
+    for i in range(len(units) + LAGS[-1]):
+        for lag, name in reversed(tuple(zip(LAGS, "XZSFR"))):
+            if 0 <= i - lag < len(units):
+                order.append((name, i - lag))
+        if i == 0:
+            order.append(("K", 0))
+        if i == len(units) - 1:
+            order.append(("L", 0))
+    return order
 
 
 def plan_of(blocks, chunks):
-    if (blocks, chunks) == (3, 3):
-        return TUNED
     return [(b, c) for c in range(chunks) for b in range(blocks)]
 
 
@@ -496,25 +504,22 @@
         while keyed[0] < count:
             loss = next_keys(loss)
             for b in range(1, len(blocks)):
-                if min(AFTER_KEYS + b - 1, chunks) == keyed[0]:
+                if min(SEND_AFTER[min(b, 2)], chunks) == keyed[0]:
                     n_send(b)
         return loss
     loss = keys_and_columns(loss, min(KEYS_AHEAD, chunks))
-    stages = tuple(zip(LAGS, (stage_x, stage_z, stage_sum, stage_far, stage_relay)))
-    if not X_FIRST:
-        stages = stages[::-1]
-    for i in range(len(units) + LAGS[-1]):
-        if i == KEYS_STEP:
+    stages = {"X": stage_x, "Z": stage_z, "S": stage_sum, "F": stage_far, "R": stage_relay}
+    for name, i in order_of(units):
+        if name == "K":
             loss = keys_and_columns(loss, chunks)
-        for lag, stage in stages:
-            if 0 <= i - lag < len(units) and units[i - lag]:
-                if not lag:
-                    ready(*units[i])
-                stage(*units[i - lag])
-        if i == len(units) - 1:
+        elif name == "L":
             from_members(loss_m, loss_s, loss_r)
             loss_g[p] = total_of(loss_m, members)
             to_groups(loss_g, lossg_s, lossg_r)
+        else:
+            if name == "X":
+                ready(*units[i])
+            stages[name](*units[i])
     from_groups(loss_g, lossg_s, lossg_r)
     loss_out[0, 0] = (total_of(loss_g, groups) / (2.0 * kv * total))[0, 0]
     for unit in units:

time: 104 us -> 115 us (1.11)
  Pallas kernels: 95.8 us -> 106 us
    pallas_call x1, Pallas kernels: 95.8 us -> 106 us  [body(): pl.pallas_call(functools.partial(kernel, members, groups, width, chunks,...]
where the time goes in v3:
time: 115 us
  Pallas kernels  106 us (92%)
  other arithmetic  4.58 us (4%)
  between operations  3.84 us (3%)
    pallas_call x1, Pallas kernels, body(): pl.pallas_call(functools.partial(kernel, members, groups, width, chunks,...  106 us
    reduce_sum x1, other arithmetic, body(): grad_gain = jnp.sum(grad_key * w_key.astype(F32), axis=1) / gains  3.97 us

profile of v3, /device:TPU:0, one launch (start us, length us, event | category | flops | bytes accessed | tf_op | source)
XLA Modules:
  0.0 114.7 jit_solution(6538939409537125264)
XLA Ops:
  0.6 0.0 copy-start
  2.1 106.3 %shard_map.85 = (bf16[1280,768]{1,0:T(8,128)(2,1)}, f32[1,1]{1,0:T(1,128)}) custom-call(s32[1]{0:T(128)S(6)} %copy.10.live_rows, s32[1,1]{1,0:T(1,128)S(6)} %copy.11.alive, bf16[256,5120]{1,0:T(8,128)(2,1)} %hidden_in.1, bf16[256,768]{1,0:T(8,128)(2,1)} %teacher.1, bf16[1280]{0:T(1024)(128)(2,1)} %gains.1, bf16[1280,768]{1,0:T(8,128)(2,1)} %w_in.1), custom_call_target="tpu_custom_call" | custom-call | tf_op jit(solution)/shard_map/pallas_call | solution.py:569
  108.4 0.0 copy-done
  108.4 0.0 copy-start.1
  108.4 4.0 %multiply_reduce_fusion = (f32[1280]{0:T(1024)S(1)}, f32[1280,768]{1,0:T(8,128)}) fusion(bf16[1280,768]{1,0:T(8,128)(2,1)S(1)} %copy-done, bf16[1280,768]{1,0:T(8,128)(2,1)} %get-tuple-element.6), kind=kLoop, calls=%fused_computation | loop fusion | flops 3930880 | bytes 7869440 | tf_op jit(solution)/shard_map/reduce_sum | solution.py:614
  112.4 0.0 copy-done.1
  112.4 0.6 convert_divide_fusion
Async XLA Ops:
  0.6 107.8 %copy-start = (bf16[1280,768]{1,0:T(8,128)(2,1)S(1)}, bf16[1280,768]{1,0:T(8,128)(2,1)}, u32[]{:S(2)}) copy-start(bf16[1280,768]{1,0:T(8,128)(2,1)} %w_in.1) | copy-start | bytes 5898244
  108.4 4.0 %copy-start.1 = (bf16[1280]{0:T(1024)(128)(2,1)S(1)}, bf16[1280]{0:T(1024)(128)(2,1)}, u32[]{:S(2)}) copy-start(bf16[1280]{0:T(1024)(128)(2,1)} %gains.1) | copy-start | bytes 7684

commit v4 on v3

--- a/solution.py
+++ b/solution.py
@@ -46,7 +46,9 @@
 
 
 def plan_of(blocks, chunks):
-    return [(b, c) for c in range(chunks) for b in range(blocks)]
+    early = max(blocks - 1, 1)
+    first = [(b, c) for c in range(chunks) for b in range(early)]
+    return first + [(b, c) for b in range(early, blocks) for c in range(chunks)]
 
 
 def paired(index, k, size):

time: 115 us -> 102 us (0.89)
  Pallas kernels: 106 us -> 93.2 us
    pallas_call x1, Pallas kernels: 106 us -> 93.2 us  [body(): pl.pallas_call(functools.partial(kernel, members, groups, width, chunks,...]
where the time goes in v4:
time: 102 us
  Pallas kernels  93.2 us (91%)
  other arithmetic  4.58 us (4%)
  between operations  3.84 us (4%)
    pallas_call x1, Pallas kernels, body(): pl.pallas_call(functools.partial(kernel, members, groups, width, chunks,...  93.2 us
    reduce_sum x1, other arithmetic, body(): grad_gain = jnp.sum(grad_key * w_key.astype(F32), axis=1) / gains  3.97 us

profile of v4, /device:TPU:0, one launch (start us, length us, event | category | flops | bytes accessed | tf_op | source)
XLA Modules:
  0.0 101.6 jit_solution(7956834542730219185)
XLA Ops:
  0.6 0.0 copy-start
  2.1 93.2 %shard_map.85 = (bf16[1280,768]{1,0:T(8,128)(2,1)}, f32[1,1]{1,0:T(1,128)}) custom-call(s32[1]{0:T(128)S(6)} %copy.10.live_rows, s32[1,1]{1,0:T(1,128)S(6)} %copy.11.alive, bf16[256,5120]{1,0:T(8,128)(2,1)} %hidden_in.1, bf16[256,768]{1,0:T(8,128)(2,1)} %teacher.1, bf16[1280]{0:T(1024)(128)(2,1)} %gains.1, bf16[1280,768]{1,0:T(8,128)(2,1)} %w_in.1), custom_call_target="tpu_custom_call" | custom-call | tf_op jit(solution)/shard_map/pallas_call | solution.py:571
  95.3 0.0 copy-done
  95.3 0.0 copy-start.1
  95.3 4.0 %multiply_reduce_fusion = (f32[1280]{0:T(1024)S(1)}, f32[1280,768]{1,0:T(8,128)}) fusion(bf16[1280,768]{1,0:T(8,128)(2,1)S(1)} %copy-done, bf16[1280,768]{1,0:T(8,128)(2,1)} %get-tuple-element.6), kind=kLoop, calls=%fused_computation | loop fusion | flops 3930880 | bytes 7869440 | tf_op jit(solution)/shard_map/reduce_sum | solution.py:616
  99.3 0.0 copy-done.1
  99.3 0.6 convert_divide_fusion
Async XLA Ops:
  0.6 94.6 %copy-start = (bf16[1280,768]{1,0:T(8,128)(2,1)S(1)}, bf16[1280,768]{1,0:T(8,128)(2,1)}, u32[]{:S(2)}) copy-start(bf16[1280,768]{1,0:T(8,128)(2,1)} %w_in.1) | copy-start | bytes 5898244
  95.3 4.0 %copy-start.1 = (bf16[1280]{0:T(1024)(128)(2,1)S(1)}, bf16[1280]{0:T(1024)(128)(2,1)}, u32[]{:S(2)}) copy-start(bf16[1280]{0:T(1024)(128)(2,1)} %gains.1) | copy-start | bytes 7684

commit v5 on v4

--- a/solution.py
+++ b/solution.py
@@ -212,7 +212,7 @@
             send(spot, spot, wz_s.at[i, e], wz_r.at[i, e], z_pair, s)
 
     def z_first(c):
-        return c % 2 == 0
+        return c % 2 == 1
 
     @scoped
     def w_spread(c):

time: 102 us -> 102 us (level)
  no operation moved by 1% of the time
where the time goes in v5:
time: 102 us; the launch traced here: 101 us
  Pallas kernels  92.9 us (91%)
  other arithmetic  4.58 us (4%)
  between operations  3.84 us (4%)
    pallas_call x1, Pallas kernels, body(): pl.pallas_call(functools.partial(kernel, members, groups, width, chunks,...  92.9 us
    reduce_sum x1, other arithmetic, body(): grad_gain = jnp.sum(grad_key * w_key.astype(F32), axis=1) / gains  3.97 us

profile of v5, /device:TPU:0, one launch (start us, length us, event | category | flops | bytes accessed | tf_op | source)
XLA Modules:
  0.0 101.3 jit_solution(9012509448017323628)
XLA Ops:
  0.6 0.0 copy-start
  2.1 92.9 %shard_map.85 = (bf16[1280,768]{1,0:T(8,128)(2,1)}, f32[1,1]{1,0:T(1,128)}) custom-call(s32[1]{0:T(128)S(6)} %copy.10.live_rows, s32[1,1]{1,0:T(1,128)S(6)} %copy.11.alive, bf16[256,5120]{1,0:T(8,128)(2,1)} %hidden_in.1, bf16[256,768]{1,0:T(8,128)(2,1)} %teacher.1, bf16[1280]{0:T(1024)(128)(2,1)} %gains.1, bf16[1280,768]{1,0:T(8,128)(2,1)} %w_in.1), custom_call_target="tpu_custom_call" | custom-call | tf_op jit(solution)/shard_map/pallas_call | solution.py:571
  94.9 0.0 copy-done
  95.0 0.0 copy-start.1
  95.0 4.0 %multiply_reduce_fusion = (f32[1280]{0:T(1024)S(1)}, f32[1280,768]{1,0:T(8,128)}) fusion(bf16[1280,768]{1,0:T(8,128)(2,1)S(1)} %copy-done, bf16[1280,768]{1,0:T(8,128)(2,1)} %get-tuple-element.6), kind=kLoop, calls=%fused_computation | loop fusion | flops 3930880 | bytes 7869440 | tf_op jit(solution)/shard_map/reduce_sum | solution.py:616
  98.9 0.0 copy-done.1
  98.9 0.6 convert_divide_fusion
Async XLA Ops:
  0.6 94.3 %copy-start = (bf16[1280,768]{1,0:T(8,128)(2,1)S(1)}, bf16[1280,768]{1,0:T(8,128)(2,1)}, u32[]{:S(2)}) copy-start(bf16[1280,768]{1,0:T(8,128)(2,1)} %w_in.1) | copy-start | bytes 5898244
  95.0 4.0 %copy-start.1 = (bf16[1280]{0:T(1024)(128)(2,1)S(1)}, bf16[1280]{0:T(1024)(128)(2,1)}, u32[]{:S(2)}) copy-start(bf16[1280]{0:T(1024)(128)(2,1)} %gains.1) | copy-start | bytes 7684
